TPU v7x, 32 devices: a whole 2x2x4 slice. The times are simulated.
32 devices in a mesh: node: 8 (over z, x), rep: 4 (over y, core).
Axes of the slice: x: 2, y: 2, z: 4, core: 2. Of those that a mesh axis runs over, the one named last changes fastest.
Arguments:
- features: bfloat16 [163840, 256], P('node'), may hold values from -6 to 6
- w_in: bfloat16 [256, 256], replicated, may hold values from -0.375 to 0.375
- w_out: bfloat16 [256, 256], replicated, may hold values from -0.375 to 0.375
- pos_src: int32 [8, 4, 8, 2], P('node', 'rep'), may hold values from 0 to 159
- pos_dst: int32 [8, 4, 8, 2], P('node', 'rep'), may hold values from 0 to 159
- counts: int32 [8, 4, 8], P('node', 'rep'), may hold values from 1 to 2, as said below
- neg_blocks: int32 [8, 2], P('node'), may hold values from 0 to 159
- neg_pick: int32 [8, 4, 8, 2], P('node', 'rep'), may hold values from 0 to 15
Outputs:
- pos_scores: float32 [8, 4, 8, 2, 128], P('node', 'rep')
- neg_term: float32 [8, 4, 8, 2, 128], P('node', 'rep')
- loss: float32 [], replicated
Inputs may be any that keep to these rules, and one draw needn't show every extreme that they name: `counts`: each entry is at most 2; in every draw one owner receives 2 live slots from every device.
All inputs are finite; a program needn't handle non-finite values.
Results may differ from a plain program's by a relative error of at most 0.0027.
Values may be sent and summed in bfloat16 or wider, within the bound.
A program may use at most 192 MiB of HBM per device.

v0:
```python
import jax
import jax.numpy as jnp
from jax import lax
from jax.sharding import PartitionSpec as P

BLK = 128


def encode(rows_in, w_in, w_out):
    hidden = jax.nn.silu(jnp.dot(rows_in, w_in, preferred_element_type=jnp.float32)).astype(
        jnp.bfloat16
    )
    return jnp.dot(hidden, w_out, preferred_element_type=jnp.float32).astype(jnp.bfloat16)


def shards(features, w_in, w_out, pos_src, pos_dst, counts, neg_blocks, neg_pick):
    rows, width = features.shape
    owners = pos_dst.shape[2]
    slots = pos_dst.shape[3]
    embed = encode(features, w_in, w_out)
    blocks = embed.reshape(rows // BLK, BLK, width)
    asked_ids = pos_dst.reshape(owners, slots)
    reply = jnp.take(
        blocks, lax.all_to_all(asked_ids, "node", split_axis=0, concat_axis=0, tiled=True), axis=0
    )
    fetched = lax.all_to_all(reply, "node", split_axis=0, concat_axis=0, tiled=True)
    offered = jnp.take(blocks, neg_blocks.reshape(-1), axis=0)
    pool = lax.all_gather(offered, "node", axis=0, tiled=True)
    source = jnp.take(blocks, pos_src.reshape(-1), axis=0).reshape(owners, slots, BLK, width)
    cand = jnp.take(pool, neg_pick.reshape(-1), axis=0).reshape(owners, slots, BLK, width)
    scale = 1.0 / width**0.5
    raw_pos = (
        jnp.einsum("ocbd,ocbd->ocb", source, fetched, preferred_element_type=jnp.float32) * scale
    )
    scores = jnp.einsum("ocbd,ocsd->ocbs", source, cand, preferred_element_type=jnp.float32) * scale
    live = jnp.arange(slots, dtype=jnp.int32)[None, :] < counts.reshape(owners, 1)
    livex = live[..., None]
    pos_out = jnp.where(livex, raw_pos, 0.0)
    neg_out = jnp.where(livex, jnp.mean(jax.nn.softplus(scores), axis=-1), 0.0)
    pos_loss = jnp.sum(jnp.where(livex, jax.nn.softplus(-raw_pos), 0.0))
    totals = lax.psum(
        (pos_loss, jnp.sum(neg_out), jnp.sum(counts).astype(jnp.float32)), ("node", "rep")
    )
    loss = (totals[0] + totals[1]) / (BLK * totals[2])
    return (
        pos_out.reshape(1, 1, owners, slots, BLK),
        neg_out.reshape(1, 1, owners, slots, BLK),
        loss,
    )


def solution(mesh):
    return jax.shard_map(
        shards,
        mesh=mesh,
        in_specs=(
            P("node", None),
            P(),
            P(),
            P("node", "rep", None, None),
            P("node", "rep", None, None),
            P("node", "rep", None),
            P("node", None),
            P("node", "rep", None, None),
        ),
        out_specs=(P("node", "rep", None, None, None), P("node", "rep", None, None, None), P()),
        check_vma=False,
    )
```

profile of v0, /device:TPU:0, one launch (start us, length us, event | category | flops | bytes accessed | tf_op | source)
XLA Modules:
  0.0 137.5 jit_solution(16845520026060009428)
XLA Ops:
  7.2 1.4 %copy.25 = s32[8,1,2]{2,1,0:T(1,128)} copy(s32[8,1,2]{0,2,1:T(2,128)} %bitcast.44) | data formatting | bytes 128 | tf_op jit(solution)/shard_map/all_to_all | solution.py:24
  8.6 7.3 %all-to-all-start = ((s32[8,1,2]{2,1,0:T(1,128)}), s32[8,1,2]{2,1,0:T(1,128)S(1)}, u32[]{:S(2)}, u32[]{:S(2)}) async-start(s32[8,1,2]{2,1,0:T(1,128)} %copy.25), calls=%async_computation | async-start | bytes 8192 | tf_op jit(solution)/shard_map/all_to_all | solution.py:24
  15.9 0.7 fusion.8
  16.5 0.7 compare_and_fusion
  17.3 10.9 %convolution_convert_fusion = bf16[20480,256]{1,0:T(8,128)(2,1)} fusion(bf16[256,256]{1,0:T(8,128)(2,1)S(1)} %copy-done, bf16[20480,256]{1,0:T(8,128)(2,1)} %param.8, bf16[256,256]{1,0:T(8,128)(2,1)} %param.9), kind=kOutput, calls=%fused_computation.4 | convolution fusion | flops 5400166400 | bytes 21233664 | tf_op jit(solution)/shard_map/dot_general | solution.py:13
  28.2 4.5 %gather_fusion.2 = bf16[2,128,256]{2,1,0:T(8,128)(2,1)S(1)} fusion(bf16[160,128,256]{2,1,0:T(8,128)(2,1)} %bitcast.41, s32[1024]{0:T(1024)S(1)} %pad_clamp_fusion.1), kind=kCustom, calls=%fused_computation.2 | custom fusion | bytes 262152 | tf_op jit(solution)/shard_map/jit(_take)/gather | solution.py:27
  32.7 0.7 broadcast_select_fusion.3
  33.5 0.6 reduce_sum.39
  34.8 0.1 copy.24
  35.0 0.1 copy.27
  35.2 4.6 %gather_fusion.1 = bf16[16,128,256]{2,1,0:T(8,128)(2,1)S(1)} fusion(bf16[160,128,256]{2,1,0:T(8,128)(2,1)} %bitcast.42, s32[1024]{0:T(1024)S(1)} %pad_clamp_fusion.2), kind=kCustom, calls=%fused_computation.1 | custom fusion | bytes 2097216 | tf_op jit(solution)/shard_map/jit(_take)/gather | solution.py:23
  39.8 1.1 broadcast_select_fusion
  41.0 6.0 %all-to-all-start.1 = ((bf16[8,2,128,256]{3,2,1,0:T(8,128)(2,1)}), bf16[8,2,128,256]{3,2,1,0:T(8,128)(2,1)S(1)}, u32[]{:S(2)}, u32[]{:S(2)}) async-start(bf16[8,2,128,256]{3,2,1,0:T(8,128)(2,1)} %broadcast_select_fusion), calls=%async_computation.1 | async-start | bytes 2097152 | tf_op jit(solution)/shard_map/all_to_all | solution.py:26
  46.9 0.1 copy.23
  47.1 0.1 copy.30
  47.4 4.6 %gather_fusion = bf16[16,128,256]{2,1,0:T(8,128)(2,1)S(1)} fusion(bf16[160,128,256]{2,1,0:T(8,128)(2,1)} %bitcast.43, s32[1024]{0:T(1024)S(1)} %pad_clamp_fusion.3), kind=kCustom, calls=%fused_computation | custom fusion | bytes 2097216 | tf_op jit(solution)/shard_map/jit(_take)/gather | solution.py:29
  52.1 30.7 %all-gather.2.cloned.1.call-done = bf16[16,128,256]{2,1,0:T(8,128)(2,1)} async-done(((bf16[2,128,256]{2,1,0:T(8,128)(2,1)}), bf16[16,128,256]{2,1,0:T(8,128)(2,1)}) %all-gather.2.cloned.1.call-update) | async-done | bytes 1048592 | tf_op jit(solution)/shard_map/all_gather | solution.py:28
  82.8 1.8 %gather_fusion.3 = bf16[16,128,256]{2,1,0:T(8,128)(2,1)S(1)} fusion(bf16[16,128,256]{2,1,0:T(8,128)(2,1)} %all-gather.2.cloned.1.call-done, s32[1024]{0:T(1024)S(1)} %pad_clamp_fusion), kind=kCustom, calls=%fused_computation.3 | custom fusion | bytes 2097216 | tf_op jit(solution)/shard_map/jit(_take)/gather | solution.py:30
  84.7 0.5 fusion.4
  85.2 0.6 select_reduce_fusion
  85.9 0.5 fusion
  86.4 1.3 select_reduce_fusion.1
  89.0 0.7 bitcast_select_fusion
  89.7 38.6 %all-reduce = (f32[]{:T(128)}, f32[]{:T(128)}) all-reduce(f32[]{:T(128)S(6)} %add.94, f32[]{:T(128)S(6)} %convert_element_type.11), channel_id=1, replica_groups=mesh['node'=8,'rep'=4] {'node','rep'}, use_global_device_ids=true, to_apply=%region_2.3 | all-reduce | flops 2 | bytes 16 | tf_op jit(solution)/shard_map/psum | solution.py:41
  (29 shorter events, 0.7 us)
Async XLA Ops:
  7.2 10.1 %copy-start = (bf16[256,256]{1,0:T(8,128)(2,1)S(1)}, bf16[256,256]{1,0:T(8,128)(2,1)}, u32[]{:S(2)}) copy-start(bf16[256,256]{1,0:T(8,128)(2,1)} %param.10) | copy-start | bytes 393220
  8.6 26.3 %all-to-all-start = ((s32[8,1,2]{2,1,0:T(1,128)}), s32[8,1,2]{2,1,0:T(1,128)S(1)}, u32[]{:S(2)}, u32[]{:S(2)}) async-start(s32[8,1,2]{2,1,0:T(1,128)} %copy.25), calls=%async_computation | async-start | bytes 8192 | tf_op jit(solution)/shard_map/all_to_all | solution.py:24
  15.8 67.0 %all-gather.2.cloned.1.call-start = ((), (), s32[]{:S(2)}) async-start(), calls=%async_computation.2 | async-start | bytes 1179648 | tf_op jit(solution)/shard_map/all_gather | solution.py:28
  17.2 16.3 %copy-start.3 = (s32[1,1,8]{2,1,0:T(1,128)S(1)}, s32[1,1,8]{2,1,0:T(1,128)}, u32[]{:S(2)}) copy-start(s32[1,1,8]{2,1,0:T(1,128)} %param.13) | copy-start | bytes 100
  17.2 17.5 %copy-start.1 = (s32[1,1,8,2]{2,3,1,0:T(2,128)S(1)}, s32[1,1,8,2]{2,3,1,0:T(2,128)}, u32[]{:S(2)}) copy-start(s32[1,1,8,2]{2,3,1,0:T(2,128)} %param.11) | copy-start | bytes 196
  17.2 29.8 %copy-start.2 = (s32[1,1,8,2]{2,3,1,0:T(2,128)S(1)}, s32[1,1,8,2]{2,3,1,0:T(2,128)}, u32[]{:S(2)}) copy-start(s32[1,1,8,2]{2,3,1,0:T(2,128)} %param.15) | copy-start | bytes 196
  41.0 44.9 %all-to-all-start.1 = ((bf16[8,2,128,256]{3,2,1,0:T(8,128)(2,1)}), bf16[8,2,128,256]{3,2,1,0:T(8,128)(2,1)S(1)}, u32[]{:S(2)}, u32[]{:S(2)}) async-start(bf16[8,2,128,256]{3,2,1,0:T(8,128)(2,1)} %broadcast_select_fusion), calls=%async_computation.1 | async-start | bytes 2097152 | tf_op jit(solution)/shard_map/all_to_all | solution.py:26
Sparse Core Ops, SparseCore 0:
  33.6 49.2 all-gather.1
where the time goes:
time: 138 us
  blocking collectives  38.6 us (28%)
  waiting for transfers between devices  30.7 us (22%)
  between operations  18.6 us (13%)
  local copies, waits for them, and re-layouts  17.8 us (13%)
  starting transfers between devices  13.3 us (10%)
  matrix products  11.5 us (8%)
  other arithmetic  7.07 us (5%)
    psum x1, blocking collectives, shards(): lax.psum((pos_loss, jnp.sum(neg_out), jnp.sum(counts).astype(jnp.float32)...  38.6 us
    all_gather x1, waiting for transfers between devices, shards(): pool = lax.all_gather(offered, 'node', axis=0, tiled=True)  30.7 us
    dot_general x1, matrix products, encode(): jnp.dot(hidden, w_out, preferred_element_type=jnp.float32)  10.9 us
    all_to_all x1, starting transfers between devices, shards(): lax.all_to_all(asked_ids, 'node', split_axis=0, concat_axis=0, tiled=True)  7.28 us
    all_to_all x1, starting transfers between devices, shards(): lax.all_to_all(reply, 'node', split_axis=0, concat_axis=0, tiled=True)  5.95 us
    gather x1, local copies, waits for them, and re-layouts, shards(): jnp.take(blocks, pos_src.reshape(-1), axis=0)  4.61 us
    gather x1, local copies, waits for them, and re-layouts, shards(): jnp.take(blocks, lax.all_to_all(asked_ids, 'node', split_axis=0, concat_a...  4.59 us
    gather x1, local copies, waits for them, and re-layouts, shards(): offered = jnp.take(blocks, neg_blocks.reshape(-1), axis=0)  4.53 us
  transfers between devices with their start and end apart: 3, of which 1 were waited for; matrix products, arithmetic and copies ran while one was open for 24% of the time, Pallas kernels for 0%

commit v1 on v0

--- a/solution.py
+++ b/solution.py
@@ -25,7 +25,12 @@
     )
     fetched = lax.all_to_all(reply, "node", split_axis=0, concat_axis=0, tiled=True)
     offered = jnp.take(blocks, neg_blocks.reshape(-1), axis=0)
-    pool = lax.all_gather(offered, "node", axis=0, tiled=True)
+    ring = [offered]
+    for hop in range(7):
+        ring.append(lax.ppermute(ring[-1], "node", [(dev, (dev + 1) % 8) for dev in range(8)]))
+    pool = jnp.roll(
+        jnp.concatenate(ring[::-1], axis=0), (lax.axis_index("node") + 1) * ring[0].shape[0], axis=0
+    )
     source = jnp.take(blocks, pos_src.reshape(-1), axis=0).reshape(owners, slots, BLK, width)
     cand = jnp.take(pool, neg_pick.reshape(-1), axis=0).reshape(owners, slots, BLK, width)
     scale = 1.0 / width**0.5

time: 138 us -> 149 us (1.080)
  waiting for transfers between devices: 30.7 us -> 52.1 us
  between operations: 18.6 us -> 5.29 us
  starting transfers between devices: 13.3 us -> 15.4 us
    ppermute x0 -> x7, waiting for transfers between devices: none -> 38.9 us  [shards(): lax.ppermute(ring[-1], 'node', [(dev, (dev + 1) % 8) for dev in range(8)])]
    all_gather x1 -> x0, waiting for transfers between devices: 30.7 us -> none  [shards(): pool = lax.all_gather(offered, 'node', axis=0, tiled=True)]
    all_to_all x1, waiting for transfers between devices: 0.01 us -> 13.2 us  [shards(): lax.all_to_all(reply, 'node', split_axis=0, concat_axis=0, tiled=True)]
    ppermute x0 -> x7, starting transfers between devices: none -> 2.09 us  [shards(): lax.ppermute(ring[-1], 'node', [(dev, (dev + 1) % 8) for dev in range(8)])]
  transfers between devices with their start and end apart: 3 -> 9, of which waited for: 1 -> 7; matrix products, arithmetic and copies ran while one was open for 24% -> 23% of each run, Pallas kernels for 0% -> 0%
where the time goes in v1:
time: 149 us; the launch traced here: 148 us
  waiting for transfers between devices  52.1 us (35%)
  blocking collectives  37.6 us (25%)
  local copies, waits for them, and re-layouts  18.5 us (12%)
  starting transfers between devices  15.4 us (10%)
  matrix products  12.7 us (9%)
  other arithmetic  6.58 us (4%)
  between operations  5.29 us (4%)
    ppermute x7, waiting for transfers between devices, shards(): lax.ppermute(ring[-1], 'node', [(dev, (dev + 1) % 8) for dev in range(8)])  38.9 us
    psum x1, blocking collectives, shards(): lax.psum((pos_loss, jnp.sum(neg_out), jnp.sum(counts).astype(jnp.float32)...  37.6 us
    all_to_all x1, waiting for transfers between devices, shards(): lax.all_to_all(reply, 'node', split_axis=0, concat_axis=0, tiled=True)  13.2 us
    dot_general x1, matrix products, encode(): jnp.dot(hidden, w_out, preferred_element_type=jnp.float32)  10.9 us
    all_to_all x1, starting transfers between devices, shards(): lax.all_to_all(asked_ids, 'node', split_axis=0, concat_axis=0, tiled=True)  7.28 us
    all_to_all x1, starting transfers between devices, shards(): lax.all_to_all(reply, 'node', split_axis=0, concat_axis=0, tiled=True)  6.01 us
    gather x1, local copies, waits for them, and re-layouts, shards(): jnp.take(blocks, lax.all_to_all(asked_ids, 'node', split_axis=0, concat_a...  4.59 us
    gather x1, local copies, waits for them, and re-layouts, shards(): jnp.take(blocks, pos_src.reshape(-1), axis=0)  4.59 us
  transfers between devices with their start and end apart: 9, of which 7 were waited for; matrix products, arithmetic and copies ran while one was open for 23% of the time, Pallas kernels for 0%

profile of v1, /device:TPU:0, one launch (start us, length us, event | category | flops | bytes accessed | tf_op | source)
XLA Modules:
  0.0 148.1 jit_solution(16190937981284827553)
XLA Ops:
  0.6 1.4 copy.25
  2.0 7.3 %all-to-all-start = ((s32[8,1,2]{2,1,0:T(1,128)}), s32[8,1,2]{2,1,0:T(1,128)S(1)}, u32[]{:S(2)}, u32[]{:S(2)}) async-start(s32[8,1,2]{2,1,0:T(1,128)} %copy.25), calls=%async_computation | async-start | bytes 8192 | tf_op jit(solution)/shard_map/all_to_all | solution.py:24
  9.3 0.7 compare_and_fusion
  10.0 0.7 fusion.8
  10.6 0.8 copy.31
  11.5 10.9 %convolution_convert_fusion = bf16[20480,256]{1,0:T(8,128)(2,1)} fusion(bf16[256,256]{1,0:T(8,128)(2,1)S(1)} %copy-done, bf16[20480,256]{1,0:T(8,128)(2,1)} %param.8, bf16[256,256]{1,0:T(8,128)(2,1)} %param.9), kind=kOutput, calls=%fused_computation.4 | convolution fusion | flops 5400166400 | bytes 21233664 | tf_op jit(solution)/shard_map/dot_general | solution.py:13
  22.4 4.5 %gather_fusion.2 = bf16[2,128,256]{2,1,0:T(8,128)(2,1)S(1)} fusion(bf16[160,128,256]{2,1,0:T(8,128)(2,1)} %bitcast.41, s32[1024]{0:T(1024)S(1)} %get-tuple-element.11), kind=kCustom, calls=%fused_computation.2 | custom fusion | bytes 262152 | tf_op jit(solution)/shard_map/jit(_take)/gather | solution.py:27
  27.1 2.1 %collective-permute-start = (bf16[2,128,256]{2,1,0:T(8,128)(2,1)S(1)}, bf16[2,128,256]{2,1,0:T(8,128)(2,1)S(1)}, u32[]{:S(2)}, u32[]{:S(2)}) collective-permute-start(bf16[2,128,256]{2,1,0:T(8,128)(2,1)S(1)} %broadcast_select_fusion.3), channel_id=1, source_target_pairs={{0,4},{4,8},{8,12},{12,16},{16,20},{20,24},{24,28},{28,0},{1,5},{5... | collective-permute-start | bytes 393224 | tf_op jit(solution)/shard_map/ppermute | solution.py:30
  30.7 4.1 %collective-permute-done = bf16[2,128,256]{2,1,0:T(8,128)(2,1)S(1)} collective-permute-done((bf16[2,128,256]{2,1,0:T(8,128)(2,1)S(1)}, bf16[2,128,256]{2,1,0:T(8,128)(2,1)S(1)}, u32[]{:S(2)}, u32[]{:S(2)}) %collective-permute-start) | collective-permute-done | bytes 131104 | tf_op jit(solution)/shard_map/ppermute | solution.py:30
  34.8 7.6 %collective-permute-done.1 = bf16[2,128,256]{2,1,0:T(8,128)(2,1)S(1)} collective-permute-done((bf16[2,128,256]{2,1,0:T(8,128)(2,1)S(1)}, bf16[2,128,256]{2,1,0:T(8,128)(2,1)S(1)}, u32[]{:S(2)}, u32[]{:S(2)}) %collective-permute-start.1) | collective-permute-done | bytes 131104 | tf_op jit(solution)/shard_map/ppermute | solution.py:30
  42.5 7.6 %collective-permute-done.2 = bf16[2,128,256]{2,1,0:T(8,128)(2,1)S(1)} collective-permute-done((bf16[2,128,256]{2,1,0:T(8,128)(2,1)S(1)}, bf16[2,128,256]{2,1,0:T(8,128)(2,1)S(1)}, u32[]{:S(2)}, u32[]{:S(2)}) %collective-permute-start.2) | collective-permute-done | bytes 131104 | tf_op jit(solution)/shard_map/ppermute | solution.py:30
  50.3 7.5 %collective-permute-done.3 = bf16[2,128,256]{2,1,0:T(8,128)(2,1)S(1)} collective-permute-done((bf16[2,128,256]{2,1,0:T(8,128)(2,1)S(1)}, bf16[2,128,256]{2,1,0:T(8,128)(2,1)S(1)}, u32[]{:S(2)}, u32[]{:S(2)}) %collective-permute-start.3) | collective-permute-done | bytes 131104 | tf_op jit(solution)/shard_map/ppermute | solution.py:30
  57.8 8.6 %collective-permute-done.4 = bf16[2,128,256]{2,1,0:T(8,128)(2,1)S(1)} collective-permute-done((bf16[2,128,256]{2,1,0:T(8,128)(2,1)S(1)}, bf16[2,128,256]{2,1,0:T(8,128)(2,1)S(1)}, u32[]{:S(2)}, u32[]{:S(2)}) %collective-permute-start.4) | collective-permute-done | bytes 131104 | tf_op jit(solution)/shard_map/ppermute | solution.py:30
  66.6 4.6 %gather_fusion.1 = bf16[16,128,256]{2,1,0:T(8,128)(2,1)S(1)} fusion(bf16[160,128,256]{2,1,0:T(8,128)(2,1)} %bitcast.42, s32[1024]{0:T(1024)S(1)} %get-tuple-element.12), kind=kCustom, calls=%fused_computation.1 | custom fusion | bytes 2097216 | tf_op jit(solution)/shard_map/jit(_take)/gather | solution.py:23
  71.2 3.5 %collective-permute-done.5 = bf16[2,128,256]{2,1,0:T(8,128)(2,1)S(1)} collective-permute-done((bf16[2,128,256]{2,1,0:T(8,128)(2,1)S(1)}, bf16[2,128,256]{2,1,0:T(8,128)(2,1)S(1)}, u32[]{:S(2)}, u32[]{:S(2)}) %collective-permute-start.5) | collective-permute-done | bytes 131104 | tf_op jit(solution)/shard_map/ppermute | solution.py:30
  74.8 1.1 broadcast_select_fusion
  75.9 4.6 %gather_fusion = bf16[16,128,256]{2,1,0:T(8,128)(2,1)S(1)} fusion(bf16[160,128,256]{2,1,0:T(8,128)(2,1)} %bitcast.43, s32[1024]{0:T(1024)S(1)} %get-tuple-element.13), kind=kCustom, calls=%fused_computation | custom fusion | bytes 2097216 | tf_op jit(solution)/shard_map/jit(_take)/gather | solution.py:34
  80.5 6.0 %all-to-all-start.1 = ((bf16[8,2,128,256]{3,2,1,0:T(8,128)(2,1)}), bf16[8,2,128,256]{3,2,1,0:T(8,128)(2,1)S(1)}, u32[]{:S(2)}, u32[]{:S(2)}) async-start(bf16[8,2,128,256]{3,2,1,0:T(8,128)(2,1)} %broadcast_select_fusion), calls=%async_computation.1 | async-start | bytes 2097152 | tf_op jit(solution)/shard_map/all_to_all | solution.py:26
  87.1 1.6 %gather_fusion.3 = bf16[16,128,256]{2,1,0:T(8,128)(2,1)} fusion(bf16[16,128,256]{2,1,0:T(8,128)(2,1)S(1)} %constant_dynamic-slice_fusion, s32[1024]{0:T(1024)S(1)} %get-tuple-element.10), kind=kCustom, calls=%fused_computation.3 | custom fusion | bytes 2097216 | tf_op jit(solution)/shard_map/jit(_take)/gather | solution.py:35
  88.7 1.8 %fusion.4 = (u8[2,128,128]{1,2,0:T(8,128)(4,1)S(1)}, f32[8,2,128,128]{2,3,1,0:T(8,128)S(1)}) fusion(bf16[8,2,128,256]{3,2,1,0:T(8,128)(2,1)} %bitcast.40, pred[8,2]{1,0:T(8,128)(4,1)S(1)} %copy.30, bf16[8,2,128,256]{3,2,1,0:T(8,128)(2,1)S(1)} %bitcast.37, pred[8,2]{1,0:T(8,128)(4,1)S(1)} %copy.23), kind=kOutput, calls=%fused_computation.17 | convolution fusion | flops 136806400 | bytes 3178528 | tf_op jit(solution)/shard_map/ocbd,ocsd->ocbs/dot_general | solution.py:40
  91.1 13.2 %all-to-all-done.1 = bf16[8,2,128,256]{3,2,1,0:T(8,128)(2,1)S(1)} async-done(((bf16[8,2,128,256]{3,2,1,0:T(8,128)(2,1)}), bf16[8,2,128,256]{3,2,1,0:T(8,128)(2,1)S(1)}, u32[]{:S(2)}, u32[]{:S(2)}) %all-to-all-start.1) | async-done | bytes 1048608 | tf_op jit(solution)/shard_map/all_to_all | solution.py:26
  104.8 1.3 select_reduce_fusion.1
  107.4 0.7 bitcast_select_fusion
  108.1 37.6 %all-reduce = (f32[]{:T(128)}, f32[]{:T(128)}) all-reduce(f32[]{:T(128)S(6)} %add.110, f32[]{:T(128)S(6)} %convert_element_type.11), channel_id=1, replica_groups=mesh['node'=8,'rep'=4] {'node','rep'}, use_global_device_ids=true, to_apply=%region_2.3 | all-reduce | flops 2 | bytes 16 | tf_op jit(solution)/shard_map/psum | solution.py:46
  (55 shorter events, 3.3 us)
Async XLA Ops:
  0.6 10.9 %copy-start = (bf16[256,256]{1,0:T(8,128)(2,1)S(1)}, bf16[256,256]{1,0:T(8,128)(2,1)}, u32[]{:S(2)}) copy-start(bf16[256,256]{1,0:T(8,128)(2,1)} %param.10) | copy-start | bytes 393220
  2.0 48.2 %all-to-all-start = ((s32[8,1,2]{2,1,0:T(1,128)}), s32[8,1,2]{2,1,0:T(1,128)S(1)}, u32[]{:S(2)}, u32[]{:S(2)}) async-start(s32[8,1,2]{2,1,0:T(1,128)} %copy.25), calls=%async_computation | async-start | bytes 8192 | tf_op jit(solution)/shard_map/all_to_all | solution.py:24
  11.5 17.7 %copy-start.3 = (s32[1,1,8]{2,1,0:T(1,128)S(1)}, s32[1,1,8]{2,1,0:T(1,128)}, u32[]{:S(2)}) copy-start(s32[1,1,8]{2,1,0:T(1,128)} %param.13) | copy-start | bytes 100
  11.5 18.9 %copy-start.1 = (s32[1,1,8,2]{2,3,1,0:T(2,128)S(1)}, s32[1,1,8,2]{2,3,1,0:T(2,128)}, u32[]{:S(2)}) copy-start(s32[1,1,8,2]{2,3,1,0:T(2,128)} %param.11) | copy-start | bytes 196
  11.5 23.3 %copy-start.2 = (s32[1,1,8,2]{2,3,1,0:T(2,128)S(1)}, s32[1,1,8,2]{2,3,1,0:T(2,128)}, u32[]{:S(2)}) copy-start(s32[1,1,8,2]{2,3,1,0:T(2,128)} %param.15) | copy-start | bytes 196
  27.1 7.7 %collective-permute-start = (bf16[2,128,256]{2,1,0:T(8,128)(2,1)S(1)}, bf16[2,128,256]{2,1,0:T(8,128)(2,1)S(1)}, u32[]{:S(2)}, u32[]{:S(2)}) collective-permute-start(bf16[2,128,256]{2,1,0:T(8,128)(2,1)S(1)} %broadcast_select_fusion.3), channel_id=1, source_target_pairs={{0,4},{4,8},{8,12},{12,16},{16,20},{20,24},{24,28},{28,0},{1,5},{5... | collective-permute-start | bytes 393224 | tf_op jit(solution)/shard_map/ppermute | solution.py:30
  34.8 7.7 %collective-permute-start.1 = (bf16[2,128,256]{2,1,0:T(8,128)(2,1)S(1)}, bf16[2,128,256]{2,1,0:T(8,128)(2,1)S(1)}, u32[]{:S(2)}, u32[]{:S(2)}) collective-permute-start(bf16[2,128,256]{2,1,0:T(8,128)(2,1)S(1)} %collective-permute-done), channel_id=1, source_target_pairs={{0,4},{4,8},{8,12},{12,16},{16,20},{20,24},{24,28},{28,0},{1,5},{5... | collective-permute-start | bytes 393224 | tf_op jit(solution)/shard_map/ppermute | solution.py:30
  42.5 7.7 %collective-permute-start.2 = (bf16[2,128,256]{2,1,0:T(8,128)(2,1)S(1)}, bf16[2,128,256]{2,1,0:T(8,128)(2,1)S(1)}, u32[]{:S(2)}, u32[]{:S(2)}) collective-permute-start(bf16[2,128,256]{2,1,0:T(8,128)(2,1)S(1)} %collective-permute-done.1), channel_id=1, source_target_pairs={{0,4},{4,8},{8,12},{12,16},{16,20},{20,24},{24,28},{28,0},{1,5},{5... | collective-permute-start | bytes 393224 | tf_op jit(solution)/shard_map/ppermute | solution.py:30
  50.1 7.7 %collective-permute-start.3 = (bf16[2,128,256]{2,1,0:T(8,128)(2,1)S(1)}, bf16[2,128,256]{2,1,0:T(8,128)(2,1)S(1)}, u32[]{:S(2)}, u32[]{:S(2)}) collective-permute-start(bf16[2,128,256]{2,1,0:T(8,128)(2,1)S(1)} %collective-permute-done.2), channel_id=1, source_target_pairs={{0,4},{4,8},{8,12},{12,16},{16,20},{20,24},{24,28},{28,0},{1,5},{5... | collective-permute-start | bytes 393224 | tf_op jit(solution)/shard_map/ppermute | solution.py:30
  57.8 8.6 %collective-permute-start.4 = (bf16[2,128,256]{2,1,0:T(8,128)(2,1)S(1)}, bf16[2,128,256]{2,1,0:T(8,128)(2,1)S(1)}, u32[]{:S(2)}, u32[]{:S(2)}) collective-permute-start(bf16[2,128,256]{2,1,0:T(8,128)(2,1)S(1)} %collective-permute-done.3), channel_id=1, source_target_pairs={{0,4},{4,8},{8,12},{12,16},{16,20},{20,24},{24,28},{28,0},{1,5},{5... | collective-permute-start | bytes 393224 | tf_op jit(solution)/shard_map/ppermute | solution.py:30
  66.3 8.4 %collective-permute-start.5 = (bf16[2,128,256]{2,1,0:T(8,128)(2,1)S(1)}, bf16[2,128,256]{2,1,0:T(8,128)(2,1)S(1)}, u32[]{:S(2)}, u32[]{:S(2)}) collective-permute-start(bf16[2,128,256]{2,1,0:T(8,128)(2,1)S(1)} %collective-permute-done.4), channel_id=1, source_target_pairs={{0,4},{4,8},{8,12},{12,16},{16,20},{20,24},{24,28},{28,0},{1,5},{5... | collective-permute-start | bytes 393224 | tf_op jit(solution)/shard_map/ppermute | solution.py:30
  74.8 11.8 %collective-permute-start.6 = (bf16[2,128,256]{2,1,0:T(8,128)(2,1)S(1)}, bf16[2,128,256]{2,1,0:T(8,128)(2,1)S(1)}, u32[]{:S(2)}, u32[]{:S(2)}) collective-permute-start(bf16[2,128,256]{2,1,0:T(8,128)(2,1)S(1)} %collective-permute-done.5), channel_id=1, source_target_pairs={{0,4},{4,8},{8,12},{12,16},{16,20},{20,24},{24,28},{28,0},{1,5},{5... | collective-permute-start | bytes 393224 | tf_op jit(solution)/shard_map/ppermute | solution.py:30
  80.5 23.8 %all-to-all-start.1 = ((bf16[8,2,128,256]{3,2,1,0:T(8,128)(2,1)}), bf16[8,2,128,256]{3,2,1,0:T(8,128)(2,1)S(1)}, u32[]{:S(2)}, u32[]{:S(2)}) async-start(bf16[8,2,128,256]{3,2,1,0:T(8,128)(2,1)} %broadcast_select_fusion), calls=%async_computation.1 | async-start | bytes 2097152 | tf_op jit(solution)/shard_map/all_to_all | solution.py:26
